TPU v7x, 32 devices: a whole 2x2x4 slice. The times are simulated.
32 devices in a mesh: batch: 4 (over x, core), seq: 8 (over z, y).
Axes of the slice: x: 2, y: 2, z: 4, core: 2. Of those that a mesh axis runs over, the one named last changes fastest.
Arguments:
- query: bfloat16 [8, 64, 128], P('batch'), may hold values from -300 to 300
- cache_keys: bfloat16 [8, 16384, 512], P('batch', 'seq'), may hold values from -6 to 6
- cache_values: bfloat16 [8, 16384, 512], P('batch', 'seq'), may hold values from -6 to 6
- new_keys: bfloat16 [8, 512], P('batch'), may hold values from -6 to 6
- new_values: bfloat16 [8, 512], P('batch'), may hold values from -6 to 6
- key_up: bfloat16 [512, 1024], P('seq'), may hold values from -0.25 to 0.25
- value_up: bfloat16 [512, 1024], P('seq'), may hold values from -0.25 to 0.25
- out_weight: bfloat16 [8192, 8192], P('seq', 'batch'), may hold values from -0.5 to 0.5
- lengths: int32 [8], P('batch'), may hold values from 128 to 16384, as said below
Outputs:
- mixed: bfloat16 [8, 8192], P('seq', 'batch')
Inputs may be any that keep to these rules, and one draw needn't show every extreme that they name: `lengths`: every length is a multiple of 128, at least 128; some sequence fills all 16384 slots. Slots at or beyond a sequence's length hold arbitrary finite entries that must not affect the result.
All inputs are finite; a program needn't handle non-finite values.
Results may differ from a plain program's by a relative error of at most 0.019.
Values may be sent and summed in bfloat16 or wider, within the bound.
A program may use at most 64 MiB of HBM per device.

v0:
```python
import functools

import jax
import jax.numpy as jnp
from jax import lax
from jax.experimental import pallas as pl
from jax.experimental.pallas import tpu as pltpu
from jax.sharding import PartitionSpec as P

NEGATIVE = -1e30
TOP_PRECISION = lax.Precision.HIGHEST
MESH = pl.DeviceIdType.MESH
NT = (((1,), (1,)), ((), ()))
NN = (((1,), (0,)), ((), ()))
F32 = jnp.float32
BF16 = jnp.bfloat16


def split_halves(x):
    head = x.astype(BF16)
    rest = (x - head.astype(F32)).astype(BF16)
    return jnp.concatenate([head, rest], axis=0)


def split_dot(x, y, dims):
    rows = x.shape[0]
    both = lax.dot_general(split_halves(x), y, dims, preferred_element_type=F32)
    return both[:rows] + both[rows:]


def step_kernel(
    ns, nb, lengths, query, keys, values, new_k, new_v, key_up, value_up, out_w, out,
    kbuf, vbuf, wbuf, qin, ku, nk, nv, qs, qfull, vcol, os, orecv, att, ps, pr,
    lsem, qsend, qrecv, vsend, vrecv, osend, orcv, asend, arcv, psend, prcv,
):
    me = lax.axis_index("seq")
    mb = lax.axis_index("batch")
    seqs, heads, dh = qin.shape
    cache_len = kbuf.shape[1]
    rl = ku.shape[0]
    hl = heads // ns
    kv = ku.shape[1] // dh
    group = heads // kv
    rows = seqs * hl
    scale = dh ** (-0.5)

    local = [
        pltpu.make_async_copy(query, qin, lsem.at[0]),
        pltpu.make_async_copy(key_up, ku, lsem.at[1]),
        pltpu.make_async_copy(new_k, nk, lsem.at[2]),
        pltpu.make_async_copy(new_v, nv, lsem.at[3]),
        pltpu.make_async_copy(
            value_up.at[:, pl.ds(pl.multiple_of(me * dh, 128), dh)],
            vcol.at[pl.ds(pl.multiple_of(me * rl, 8), rl)],
            lsem.at[4],
        ),
        pltpu.make_async_copy(keys.at[0], kbuf.at[0], lsem.at[5]),
        pltpu.make_async_copy(keys.at[1], kbuf.at[1], lsem.at[6]),
        pltpu.make_async_copy(values.at[0], vbuf.at[0], lsem.at[7]),
        pltpu.make_async_copy(values.at[1], vbuf.at[1], lsem.at[8]),
        pltpu.make_async_copy(out_w, wbuf, lsem.at[9]),
    ]
    for copy in local:
        copy.start()

    barrier = pltpu.get_barrier_semaphore()
    for d in range(1, ns):
        pl.semaphore_signal(
            barrier, inc=1, device_id={"seq": lax.rem(me + d, ns)}, device_id_type=MESH
        )
    for d in range(1, nb):
        pl.semaphore_signal(
            barrier, inc=1, device_id={"batch": lax.rem(mb + d, nb)}, device_id_type=MESH
        )

    local[0].wait()
    local[1].wait()
    low = lax.broadcasted_iota(jnp.int32, (group, 2 * rl), 1) < rl
    for k in range(kv):
        part = ku[:, k * dh : (k + 1) * dh]
        twice = jnp.concatenate([part, part], axis=0)
        asked = jnp.concatenate(
            [qin[b, k * group : (k + 1) * group, :].astype(F32) for b in range(seqs)], axis=0
        ).astype(BF16)
        got = lax.dot_general(asked, twice, NT, preferred_element_type=F32)
        qs[me, k * group : (k + 1) * group, :] = jnp.where(low, got[:group], got[group:])

    pl.semaphore_wait(barrier, ns - 1 + nb - 1)

    def hop(src, dst, send, recv, d, axis, target):
        return pltpu.make_async_remote_copy(
            src_ref=src, dst_ref=dst, send_sem=send.at[d], recv_sem=recv.at[d],
            device_id={axis: target}, device_id_type=MESH,
        )

    started = []
    bits = [lax.rem(lax.div(me, 1 << i), 2) for i in range((ns - 1).bit_length())]

    def across(d):
        return sum((1 - x if d >> i & 1 else x) * (1 << i) for i, x in enumerate(bits))

    def send_all(order, partner, index, axis, src_of, dst, send, recv):
        for d in order:
            copy = hop(src_of(partner(d)), dst(index), send, recv, d, axis, partner(d))
            copy.start()
            started.append(copy)

    def receive(d, partner, axis, src_of, dst, send, recv):
        hop(src_of(partner(d)), dst(partner(d)), send, recv, d, axis, partner(d)).wait_recv()

    near, far = list(range(1, ns // 2)), list(range(ns // 2, ns))
    everyone = near + far
    q_src, q_dst = (lambda t: qs.at[me]), (lambda s: qs.at[s])
    send_all(everyone, across, me, "seq", q_src, q_dst, qsend, qrecv)

    wide = lax.broadcasted_iota(jnp.int32, (heads, 2 * rl), 1) < rl
    side = lax.div(me, ns // 2)
    half_rank = rl * ns // 2

    def gathered(half):
        for pair in range(ns // 4):
            even = qs[half * (ns // 2) + 2 * pair]
            odd = qs[half * (ns // 2) + 2 * pair + 1]
            lanes = slice(pair * 2 * rl, (pair + 1) * 2 * rl)
            qfull[0, half, :, lanes] = jnp.where(wide, even, pltpu.roll(odd, rl, 1))
            qfull[1, half, :, lanes] = jnp.where(wide, pltpu.roll(even, rl, 1), odd)

    def half_scores(b, half):
        columns = pl.ds(pl.multiple_of(half * half_rank, 128), half_rank)
        return split_dot(qfull[b, half], kbuf[b, :, columns], NT)

    for d in near:
        receive(d, across, "seq", q_src, q_dst, qsend, qrecv)
    gathered(side)
    early = []
    for b in range(seqs):
        local[5 + b].wait()
        early.append(half_scores(b, side))
    for d in far:
        receive(d, across, "seq", q_src, q_dst, qsend, qrecv)
    gathered(1 - side)

    v_src = lambda t: value_up.at[:, pl.ds(pl.multiple_of(t * dh, 128), dh)]
    v_dst = lambda s: vcol.at[pl.ds(pl.multiple_of(s * rl, 8), rl)]
    send_all(everyone, across, me, "seq", v_src, v_dst, vsend, vrecv)

    positions = me * cache_len + lax.broadcasted_iota(jnp.int32, (1, cache_len), 1)
    lane = lax.broadcasted_iota(jnp.int32, (heads, 128), 1)
    o_args = []
    for b in range(seqs):
        live = positions < lengths[b]
        scores = (early[b] + half_scores(b, 1 - side)) * scale
        scores = jnp.where(live, scores, NEGATIVE)
        top = jnp.max(scores, axis=1, keepdims=True)
        terms = jnp.where(live, jnp.exp(scores - top), 0.0)
        total = jnp.sum(terms, axis=1, keepdims=True)
        local[7 + b].wait()
        sums = split_dot(terms, vbuf[b], NN)
        pieces = jnp.zeros((heads, 128), F32)
        for at, value in ((0, top), (3, total)):
            for k in range(3):
                piece = value.astype(BF16).astype(F32)
                pieces = jnp.where(lane == at + k, piece, pieces)
                value = value - piece
        packed = jnp.concatenate([sums, pieces], axis=1)
        for p in range(ns):
            os[b, p] = packed[p * hl : (p + 1) * hl].astype(BF16)
        o_args.append(
            (
                "seq", lambda t, b=b: os.at[b, t], lambda s, b=b: orecv.at[b, s],
                osend.at[b], orcv.at[b],
            )
        )
        send_all(everyone, across, me, *o_args[b])
        orecv[b, me] = os[b, me]

    local[2].wait()
    local[3].wait()
    local[4].wait()
    mine = pl.ds(pl.multiple_of(me * hl, 8), hl)
    own_query = jnp.concatenate(
        [
            jnp.concatenate([qfull[b, half, mine, :] for half in range(2)], axis=1)
            for b in range(seqs)
        ],
        axis=0,
    )

    def spread(ref):
        full = ref[...].astype(F32)
        return jnp.concatenate(
            [jnp.broadcast_to(full[b : b + 1], (hl, full.shape[1])) for b in range(seqs)], axis=0
        )

    own = jnp.sum(own_query * spread(nk), axis=1, keepdims=True) * scale
    fresh = spread(nv)

    rank = nk.shape[1]
    latents, belows = [], []
    for b in range(seqs):
        for d in near + far:
            receive(d, across, *o_args[b])
        span = slice(b * hl, (b + 1) * hl)
        notes = orecv[b, :, :, rank:].astype(F32)
        top = notes[:, :, 0:1] + notes[:, :, 1:2] + notes[:, :, 2:3]
        total = notes[:, :, 3:4] + notes[:, :, 4:5] + notes[:, :, 5:6]
        limit = jnp.maximum(jnp.max(top, axis=0), own[span])
        factor = jnp.exp(top - limit[None])
        own_weight = jnp.exp(own[span] - limit)
        latent = own_weight * fresh[span]
        for p in range(ns):
            latent = latent + factor[p] * orecv[b, p, :, :rank].astype(F32)
        latents.append(latent)
        belows.append(own_weight + jnp.sum(factor * total, axis=0))
    latent = jnp.concatenate(latents, axis=0)
    below = jnp.concatenate(belows, axis=0)
    for d in near + far:
        receive(d, across, "seq", v_src, v_dst, vsend, vrecv)
    attended = split_dot(latent, vcol[...], NN) / below
    att[pl.ds(pl.multiple_of(mb * rows, 8), rows), :] = attended.astype(BF16).astype(F32)

    def att_rows(i):
        return att.at[pl.ds(pl.multiple_of(i * rows, 8), rows)]

    def turned(d):
        return lax.rem(mb + d, nb)

    def turned_back(d):
        return lax.rem(mb + nb - d, nb)

    a_src = lambda t: att_rows(mb)
    send_all(range(1, nb), turned, mb, "batch", a_src, att_rows, asend, arcv)
    for d in range(1, nb):
        receive(d, turned_back, "batch", a_src, att_rows, asend, arcv)
    features = jnp.concatenate(
        [att[pl.ds(g, nb * seqs, stride=hl), :] for g in range(hl)], axis=1
    ).astype(BF16)
    local[9].wait()
    product = lax.dot_general(features, wbuf[...], NN, preferred_element_type=F32)
    for p in range(ns):
        ps[p] = product[p : p + 1].astype(ps.dtype)
    p_src, p_dst = (lambda t: ps.at[t]), (lambda s: pr.at[s])
    send_all(everyone, across, me, "seq", p_src, p_dst, psend, prcv)
    pr[me] = ps[me]
    for d in near + far:
        receive(d, across, "seq", p_src, p_dst, psend, prcv)
    result = pr[0].astype(F32)
    for p in range(1, ns):
        result = result + pr[p].astype(F32)
    out[...] = result.astype(out.dtype)
    for copy in started:
        copy.wait_send()


def fused_body(
    query, cache_keys, cache_values, new_keys, new_values, key_up, value_up, out_weight, lengths
):
    ns, nb = lax.axis_size("seq"), lax.axis_size("batch")
    seqs, cache_len, rank = cache_keys.shape
    heads, dh = query.shape[1:]
    hl = heads // ns
    width = out_weight.shape[1]
    sem = pltpu.SemaphoreType.DMA
    hbm = pl.BlockSpec(memory_space=pl.ANY)
    return pl.pallas_call(
        functools.partial(step_kernel, ns, nb),
        out_shape=jax.ShapeDtypeStruct((1, width), BF16),
        in_specs=[pl.BlockSpec(memory_space=pltpu.SMEM)] + [hbm] * 8,
        out_specs=pl.BlockSpec(memory_space=pltpu.VMEM),
        scratch_shapes=[
            pltpu.VMEM(cache_keys.shape, BF16),
            pltpu.VMEM(cache_values.shape, BF16),
            pltpu.VMEM(out_weight.shape, BF16),
            pltpu.VMEM(query.shape, BF16),
            pltpu.VMEM(key_up.shape, BF16),
            pltpu.VMEM(new_keys.shape, BF16),
            pltpu.VMEM(new_values.shape, BF16),
            pltpu.VMEM((ns, heads, seqs * key_up.shape[0]), F32),
            pltpu.VMEM((seqs, 2, heads, rank // 2), F32),
            pltpu.VMEM((rank, dh), BF16),
            pltpu.VMEM((seqs, ns, hl, rank + 128), BF16),
            pltpu.VMEM((seqs, ns, hl, rank + 128), BF16),
            pltpu.VMEM((nb * seqs * hl, dh), F32),
            pltpu.VMEM((ns, 1, width), BF16),
            pltpu.VMEM((ns, 1, width), BF16),
            sem((10,)),
        ]
        + [sem((ns,))] * 4
        + [sem((seqs, ns))] * 2
        + [sem((nb,))] * 2
        + [sem((ns,))] * 2,
        compiler_params=pltpu.CompilerParams(collective_id=0, has_side_effects=True),
        name="decode_step",
    )(
        lengths, query, cache_keys, cache_values, new_keys, new_values, key_up, value_up, out_weight
    )


def fits(mesh, query, cache_keys, key_up):
    ns, nb = mesh.shape["seq"], mesh.shape["batch"]
    heads, dh = query.shape[1:]
    kv = key_up.shape[1] // dh
    seqs = query.shape[0] // nb
    return (
        seqs == 2 and kv == ns and heads // kv == 8 and dh == 128
        and key_up.shape[0] // ns == 64 and query.shape[0] == ns
        and cache_keys.shape[1] // ns * cache_keys.shape[2] <= 2 ** 21
    )


def body(
    query, cache_keys, cache_values, new_keys, new_values, key_up, value_up, out_weight, lengths
):
    batch_rows, cache_len, rank_full = cache_keys.shape
    head_count, head_dimension = (query.shape[1], query.shape[2])
    kv_heads = key_up.shape[1] // head_dimension
    group_size = head_count // kv_heads
    score_scale_factor = head_dimension ** (-0.5)
    seq_index = lax.axis_index("seq")
    seq_count = lax.axis_size("seq")
    local_head_index = head_count // seq_count
    positions = seq_index * cache_len + lax.iota(jnp.int32, cache_len)
    live_mask = (positions[None, :] < lengths[:, None])[:, None, None, :]
    grouped = query.reshape(batch_rows, kv_heads, group_size, head_dimension)
    key_full, value_full = (
        lax.all_gather(key_up, "seq", axis=0, tiled=True),
        lax.all_gather(value_up, "seq", axis=0, tiled=True),
    )
    rebuilt_keys = jnp.dot(
        cache_keys.reshape(batch_rows * cache_len, rank_full),
        key_full,
        preferred_element_type=jnp.float32,
    ).reshape(batch_rows, cache_len, kv_heads, head_dimension)
    rebuilt_values = jnp.dot(
        cache_values.reshape(batch_rows * cache_len, rank_full),
        value_full,
        preferred_element_type=jnp.float32,
    ).reshape(batch_rows, cache_len, kv_heads, head_dimension)
    expanded_query = grouped.astype(jnp.float32)
    scores = (
        jnp.einsum("bkgd,blkd->bkgl", expanded_query, rebuilt_keys, precision=TOP_PRECISION)
        * score_scale_factor
    )
    fresh_key_row = jnp.dot(new_keys, key_full, preferred_element_type=jnp.float32).reshape(
        batch_rows, kv_heads, head_dimension
    )
    current_token_score = (
        jnp.einsum("phsu,phu->phs", expanded_query, fresh_key_row, precision=TOP_PRECISION)
        * score_scale_factor
    )
    new_value = jnp.dot(new_values, value_full, preferred_element_type=jnp.float32).reshape(
        batch_rows, kv_heads, head_dimension
    )
    scores = jnp.where(live_mask, scores, NEGATIVE)
    local_max = jnp.max(scores, axis=-1)
    upper_limit = jnp.maximum(lax.pmax(local_max, "seq"), current_token_score)
    softmax_terms = jnp.where(live_mask, jnp.exp(scores - upper_limit[..., None]), 0.0)
    denominator = jnp.sum(softmax_terms, axis=-1)
    totals = jnp.einsum("bkgl,blkd->bkgd", softmax_terms, rebuilt_values, precision=TOP_PRECISION)
    denominator, totals = (
        lax.psum(denominator.astype(jnp.bfloat16), "seq").astype(jnp.float32),
        lax.psum(totals.astype(jnp.bfloat16), "seq").astype(jnp.float32),
    )
    own_weight = jnp.exp(current_token_score - upper_limit)
    normalized = (totals + own_weight[..., None] * new_value[:, :, None, :]) / (
        denominator + own_weight
    )[..., None]
    normalized = normalized.reshape(batch_rows, head_count * head_dimension)
    width_local = local_head_index * head_dimension
    attended = lax.dynamic_slice_in_dim(normalized, seq_index * width_local, width_local, 1).astype(
        jnp.bfloat16
    )
    partial_out = jnp.dot(
        lax.all_gather(attended, "batch", axis=0, tiled=True),
        out_weight,
        preferred_element_type=jnp.float32,
    )
    return lax.psum_scatter(
        partial_out.astype(jnp.bfloat16), "seq", scatter_dimension=0, tiled=True
    )


def solution(mesh):
    placed = (
        P("batch", None, None),
        P("batch", "seq", None),
        P("batch", "seq", None),
        P("batch", None),
        P("batch", None),
        P("seq", None),
        P("seq", None),
        P("seq", "batch"),
        P("batch"),
    )

    def run(*args):
        chosen = fused_body if fits(mesh, args[0], args[1], args[5]) else body
        return jax.shard_map(
            chosen, mesh=mesh, in_specs=placed, out_specs=P("seq", "batch"), check_vma=False
        )(*args)

    return run
```

profile of v0, /device:TPU:0, one launch (start us, length us, event | category | flops | bytes accessed | tf_op | source)
XLA Modules:
  0.0 31.9 jit_solution(2111901689218607435)
XLA Ops:
  0.0 30.6 %decode_step.1 = bf16[1,2048]{1,0:T(2,128)(2,1)} custom-call(s32[2]{0:T(128)} %lengths.1, bf16[2,64,128]{2,1,0:T(8,128)(2,1)} %query.1, bf16[2,2048,512]{2,1,0:T(8,128)(2,1)} %keys.1, bf16[2,2048,512]{2,1,0:T(8,128)(2,1)} %values.1, bf16[2,512]{1,0:T(2,128)(2,1)} %new_k.1, bf16[2,512]{1,0:T(2,128)(2,1)} %new_v.1, bf16[64,1024]{1,0:T(8,128)(2,1)} %key_up.1, ...), custom_call_target="tpu_custom_call" | custom-call | tf_op jit(solution)/shard_map/decode_step/pallas_call | solution.py:265
  30.6 1.3 %copy.11 = bf16[1,2048]{1,0:T(2,128)(2,1)} copy(bf16[1,2048]{1,0:T(2,128)(2,1)} %decode_step.1) | data formatting | bytes 8192
where the time goes:
time: 32.1 us; the launch traced here: 31.9 us
  Pallas kernels  30.6 us (95%)
  local copies, waits for them, and re-layouts  1.3 us (4%)
    pallas_call x1, Pallas kernels, fused_body(): pl.pallas_call(functools.partial(step_kernel, ns, nb), out_shape=jax.Shap...  30.6 us
    unnamed x1, local copies, waits for them, and re-layouts  1.3 us

commit v1 on v0

v1 whole, which is shorter than its diff:
```python
import functools

import jax
import jax.numpy as jnp
from jax import lax
from jax.experimental import pallas as pl
from jax.experimental.pallas import tpu as pltpu
from jax.sharding import PartitionSpec as P

NEGATIVE = -1e30
LOG2E = 1.4426950408889634
TOP_PRECISION = lax.Precision.HIGHEST
MESH = pl.DeviceIdType.MESH
NT = (((1,), (1,)), ((), ()))
NN = (((1,), (0,)), ((), ()))
F32 = jnp.float32
BF16 = jnp.bfloat16


def split_halves(x):
    head = x.astype(BF16)
    rest = (x - head.astype(F32)).astype(BF16)
    return jnp.concatenate([head, rest], axis=0)


def split_dot(x, y, dims):
    rows = x.shape[0]
    both = lax.dot_general(split_halves(x), y, dims, preferred_element_type=F32)
    return both[:rows] + both[rows:]


def dot(x, y, dims):
    return lax.dot_general(x, y, dims, preferred_element_type=F32)


def step_kernel(
    ns, nb, lengths, query, keys, values, new_k, new_v, key_up, value_up, out_w, out,
    kbuf, vbuf, wbuf, lens, qin, ku, vu, nk, nv, qbd, qs, rhs, score, turned_terms,
    vcol, os, orecv, stats, gains, att, attf, pscr, ps, pr,
    lsem, qsend, qrecv, vsend, vrecv, usend, urecv,
    ssend, srecv, osend, orcv, asend, arcv, psend, prcv,
):
    me = lax.axis_index("seq")
    mb = lax.axis_index("batch")
    seqs, heads, dh = qin.shape
    cache_len = kbuf.shape[1]
    rl, kv_width = ku.shape
    rank = kbuf.shape[2]
    hl = heads // ns
    kv = kv_width // dh
    group = heads // kv
    rows = seqs * hl
    lanes = seqs * heads
    quarter = rl // nb

    barrier = pltpu.get_barrier_semaphore()
    for d in range(1, ns):
        pl.semaphore_signal(
            barrier, inc=1, device_id={"seq": lax.rem(me + d, ns)}, device_id_type=MESH
        )
    for d in range(1, nb):
        pl.semaphore_signal(
            barrier, inc=1, device_id={"batch": lax.rem(mb + d, nb)}, device_id_type=MESH
        )

    local = [
        pltpu.make_async_copy(src, dst, lsem.at[i])
        for i, (src, dst) in enumerate(
            [
                (key_up, ku), (query, qin), (value_up, vu), (lengths, lens),
                (new_k, nk), (new_v, nv),
                (keys.at[0], kbuf.at[0]), (keys.at[1], kbuf.at[1]),
                (values.at[0], vbuf.at[0]), (values.at[1], vbuf.at[1]),
                (out_w, wbuf),
            ]
        )
    ]
    for copy in local:
        copy.start()

    started = []
    bits = [lax.rem(lax.div(me, 1 << i), 2) for i in range((ns - 1).bit_length())]

    def across(d):
        return sum((1 - x if d >> i & 1 else x) * (1 << i) for i, x in enumerate(bits))

    def turned(d):
        return lax.rem(mb + d, nb)

    def turned_back(d):
        return lax.rem(mb + nb - d, nb)

    def hop(src, dst, send, recv, d, axis, target):
        return pltpu.make_async_remote_copy(
            src_ref=src, dst_ref=dst, send_sem=send.at[d], recv_sem=recv.at[d],
            device_id={axis: target}, device_id_type=MESH,
        )

    def send_all(order, partner, index, axis, src_of, dst, send, recv):
        for d in order:
            copy = hop(src_of(partner(d)), dst(index), send, recv, d, axis, partner(d))
            copy.start()
            started.append(copy)

    def receive(d, partner, axis, src_of, dst, send, recv):
        hop(src_of(partner(d)), dst(partner(d)), send, recv, d, axis, partner(d)).wait_recv()

    near, far = list(range(1, ns // 2)), list(range(ns // 2, ns))
    everyone = far + near

    qbd[...] = jnp.zeros(qbd.shape, F32)
    local[0].wait()
    local[1].wait()
    for b in range(seqs):
        for k in range(kv):
            at = b * heads + k * group
            qbd[at : at + group, k * dh : (k + 1) * dh] = qin[
                b, k * group : (k + 1) * group, :
            ].astype(F32)
    asked = dot(ku[...], qbd[...].astype(BF16), NT) * (dh ** (-0.5) * LOG2E)
    qs[me] = asked
    local[2].wait()
    own_rows = pl.ds(pl.multiple_of(mb * quarter, quarter), quarter)
    own_column = pl.ds(pl.multiple_of(me * dh, 128), dh)
    vcol[me, mb] = vu[own_rows, own_column]

    pl.semaphore_wait(barrier, ns - 1 + nb - 1)

    q_args = (across, "seq", lambda t: qs.at[me], lambda s: qs.at[s], qsend, qrecv)
    v_args = (
        across, "seq",
        lambda t: vu.at[own_rows, pl.ds(pl.multiple_of(t * dh, 128), dh)],
        lambda s: vcol.at[s, mb],
        vsend, vrecv,
    )

    def post(order, args, index=me):
        partner, axis, src_of, dst, send, recv = args
        send_all(order, partner, index, axis, src_of, dst, send, recv)

    def take(order, args):
        for d in order:
            receive(d, *args)

    post(everyone, q_args)
    post(everyone, v_args)

    low = lax.broadcasted_iota(jnp.int32, (1, lanes), 1) < heads
    side = lax.div(me, ns // 2)
    half_rank = rank // 2

    def swap(x):
        return pltpu.roll(x, heads, 1)

    def gathered(half):
        for j in range(ns // 2):
            s = half * (ns // 2) + j
            x = qs[s]
            head = x.astype(BF16).astype(F32)
            rest = swap(x - head)
            span = pl.ds(pl.multiple_of(s * rl, rl), rl)
            rhs[0, span, :] = jnp.where(low, head, rest).astype(BF16)
            rhs[1, span, :] = jnp.where(low, rest, head).astype(BF16)

    chunk = 512
    spans = [slice(c, c + chunk) for c in range(0, cache_len, chunk)]

    def merged(r0, r1):
        return jnp.where(low, r0, r1) + swap(jnp.where(low, r1, r0))

    def half_scores(span, half):
        columns = pl.ds(pl.multiple_of(half * half_rank, 128), half_rank)
        return merged(
            *[dot(kbuf[b, span, columns], rhs[b, columns, :], NN) for b in range(seqs)]
        )

    take(near, q_args)
    gathered(side)
    for i in (6, 7, 3):
        local[i].wait()
    for span in spans:
        score[span, :] = half_scores(span, side)
    take(far, q_args)
    gathered(1 - side)

    limits = jnp.where(low, lens[0], lens[1]) - me * cache_len
    top = jnp.full((8, lanes), 0.5 * NEGATIVE, F32)
    for span in spans:
        positions = span.start + lax.broadcasted_iota(jnp.int32, (chunk, lanes), 0)
        whole = score[span, :] + half_scores(span, 1 - side)
        whole = jnp.where(positions < limits, whole, NEGATIVE)
        score[span, :] = whole
        top = jnp.maximum(top, jnp.max(whole.reshape(chunk // 8, 8, lanes), axis=0))
    top = jnp.max(top, axis=0, keepdims=True)

    local[8].wait()
    total = jnp.zeros((8, lanes), F32)
    sums = jnp.zeros((heads, rank), F32)
    for span in spans:
        terms = jnp.exp2(score[span, :] - top).astype(BF16)
        total = total + jnp.sum(terms.astype(F32).reshape(chunk // 8, 8, lanes), axis=0)
        across_lanes = terms.T
        turned_terms[:, span] = across_lanes[heads:, :]
        sums = sums + dot(across_lanes[:heads, :], vbuf[0, span, :], NN)
    stats[me, 0:1, :] = top
    stats[me, 1:2, :] = jnp.sum(total, axis=0, keepdims=True)
    s_args = (across, "seq", lambda t: stats.at[me], lambda s: stats.at[s], ssend, srecv)
    post(everyone, s_args)

    def o_args(b):
        return (
            across, "seq", lambda t: os.at[b, t], lambda s: orecv.at[b, s],
            osend.at[b], orcv.at[b],
        )

    def share(b, sums):
        for p in range(ns):
            os[b, p] = sums[p * hl : (p + 1) * hl].astype(BF16)
        post(everyone, o_args(b))
        orecv[b, me] = os[b, me]

    share(0, sums)
    take(everyone, v_args)
    u_args = (turned, "batch", lambda t: vcol.at[:, mb], lambda s: vcol.at[:, s], usend, urecv)
    post(range(1, nb), u_args, mb)
    local[9].wait()
    share(1, dot(turned_terms[...], vbuf[1], NN))

    local[4].wait()
    local[5].wait()
    fresh = [dot(nk[...], rhs[b], NN)[b : b + 1] for b in range(seqs)]
    own = merged(*[jnp.broadcast_to(x, (8, lanes)) for x in fresh])[0:1]

    take(everyone, s_args)
    tops, totals = stats[:, 0, :], stats[:, 1, :]
    limit = jnp.maximum(jnp.max(tops, axis=0, keepdims=True), own)
    factor = jnp.exp2(tops - limit)
    own_weight = jnp.exp2(own - limit)
    below = own_weight + jnp.sum(factor * totals, axis=0, keepdims=True)
    shares = jnp.concatenate(
        [factor / below, jnp.broadcast_to(own_weight / below, (lanes - ns, lanes))], axis=0
    )
    gains[...] = shares.T

    latents = []
    for b in range(seqs):
        gain = gains[pl.ds(pl.multiple_of(b * heads + me * hl, 8), hl), :]
        take(everyone, o_args(b))
        latent = gain[:, ns : ns + 1] * nv[b : b + 1, :].astype(F32)
        for p in range(ns):
            latent = latent + gain[:, p : p + 1] * orecv[b, p].astype(F32)
        latents.append(latent)
    latent = jnp.concatenate(latents, axis=0)
    for d in range(1, nb):
        receive(d, turned_back, *u_args[1:])
    attended = split_dot(latent, vcol[...].reshape(rank, dh), NN)
    att[mb] = attended.astype(BF16)

    a_args = (turned, "batch", lambda t: att.at[mb], lambda s: att.at[s], asend, arcv)
    post(range(1, nb), a_args, mb)
    local[10].wait()
    for d in range(1, nb):
        receive(d, turned_back, *a_args[1:])
    attf[...] = att[...].reshape(nb * rows, dh).astype(F32)
    features = jnp.concatenate(
        [attf[pl.ds(g, nb * seqs, stride=hl), :] for g in range(hl)], axis=1
    ).astype(BF16)
    product = dot(features, wbuf[...], NN)
    for j in range(pscr.shape[1]):
        pscr[:, j, :] = product[:, j * 128 : (j + 1) * 128]
    for p in range(ns):
        ps[p] = pscr[p].astype(BF16)
    p_args = (across, "seq", lambda t: ps.at[t], lambda s: pr.at[s], psend, prcv)
    post(everyone, p_args)
    pr[me] = ps[me]
    take(everyone, p_args)
    result = pr[0].astype(F32)
    for p in range(1, ns):
        result = result + pr[p].astype(F32)
    out[...] = result.astype(out.dtype)
    for copy in started:
        copy.wait_send()


def fused_body(
    query, cache_keys, cache_values, new_keys, new_values, key_up, value_up, out_weight, lengths
):
    ns, nb = lax.axis_size("seq"), lax.axis_size("batch")
    seqs, cache_len, rank = cache_keys.shape
    heads, dh = query.shape[1:]
    hl = heads // ns
    rl = key_up.shape[0]
    lanes = seqs * heads
    width = out_weight.shape[1]
    dma = pltpu.SemaphoreType.DMA
    vmem = pltpu.VMEM
    hbm = pl.BlockSpec(memory_space=pl.ANY)
    mixed = pl.pallas_call(
        functools.partial(step_kernel, ns, nb),
        out_shape=jax.ShapeDtypeStruct((width // 128, 128), BF16),
        in_specs=[hbm] * 9,
        out_specs=pl.BlockSpec(memory_space=pltpu.VMEM),
        scratch_shapes=[
            vmem(cache_keys.shape, BF16),
            vmem(cache_values.shape, BF16),
            vmem(out_weight.shape, BF16),
            pltpu.SMEM(lengths.shape, jnp.int32),
            vmem(query.shape, BF16),
            vmem(key_up.shape, BF16),
            vmem(value_up.shape, BF16),
            vmem(new_keys.shape, BF16),
            vmem(new_values.shape, BF16),
            vmem((lanes, key_up.shape[1]), F32),
            vmem((ns, rl, lanes), F32),
            vmem((seqs, rank, lanes), BF16),
            vmem((cache_len, lanes), F32),
            vmem((heads, cache_len), BF16),
            vmem((ns, nb, rl // nb, dh), BF16),
            vmem((seqs, ns, hl, rank), BF16),
            vmem((seqs, ns, hl, rank), BF16),
            vmem((ns, 2, lanes), F32),
            vmem((lanes, lanes), F32),
            vmem((nb, seqs * hl, dh), BF16),
            vmem((nb * seqs * hl, dh), F32),
            vmem((ns, width // 128, 128), F32),
            vmem((ns, width // 128, 128), BF16),
            vmem((ns, width // 128, 128), BF16),
            dma((11,)),
        ]
        + [dma((ns,))] * 4
        + [dma((nb,))] * 2
        + [dma((ns,))] * 2
        + [dma((seqs, ns))] * 2
        + [dma((nb,))] * 2
        + [dma((ns,))] * 2,
        compiler_params=pltpu.CompilerParams(collective_id=0, has_side_effects=True),
        name="decode_step",
    )(
        lengths, query, cache_keys, cache_values, new_keys, new_values, key_up, value_up, out_weight
    )
    return mixed.reshape(1, width)


def fits(mesh, query, cache_keys, key_up):
    ns, nb = mesh.shape["seq"], mesh.shape["batch"]
    heads, dh = query.shape[1:]
    kv = key_up.shape[1] // dh
    seqs = query.shape[0] // nb
    return (
        seqs == 2 and kv == ns and heads // kv == 8 and heads == 64 and dh == 128 and nb == 4
        and key_up.shape[0] // ns == 64 and query.shape[0] == ns
        and cache_keys.shape[1] // ns * cache_keys.shape[2] <= 2 ** 20
        and cache_keys.shape[1] // ns % 512 == 0
    )


def body(
    query, cache_keys, cache_values, new_keys, new_values, key_up, value_up, out_weight, lengths
):
    batch_rows, cache_len, rank_full = cache_keys.shape
    head_count, head_dimension = (query.shape[1], query.shape[2])
    kv_heads = key_up.shape[1] // head_dimension
    group_size = head_count // kv_heads
    score_scale_factor = head_dimension ** (-0.5)
    seq_index = lax.axis_index("seq")
    seq_count = lax.axis_size("seq")
    local_head_index = head_count // seq_count
    positions = seq_index * cache_len + lax.iota(jnp.int32, cache_len)
    live_mask = (positions[None, :] < lengths[:, None])[:, None, None, :]
    grouped = query.reshape(batch_rows, kv_heads, group_size, head_dimension)
    key_full, value_full = (
        lax.all_gather(key_up, "seq", axis=0, tiled=True),
        lax.all_gather(value_up, "seq", axis=0, tiled=True),
    )
    rebuilt_keys = jnp.dot(
        cache_keys.reshape(batch_rows * cache_len, rank_full),
        key_full,
        preferred_element_type=jnp.float32,
    ).reshape(batch_rows, cache_len, kv_heads, head_dimension)
    rebuilt_values = jnp.dot(
        cache_values.reshape(batch_rows * cache_len, rank_full),
        value_full,
        preferred_element_type=jnp.float32,
    ).reshape(batch_rows, cache_len, kv_heads, head_dimension)
    expanded_query = grouped.astype(jnp.float32)
    scores = (
        jnp.einsum("bkgd,blkd->bkgl", expanded_query, rebuilt_keys, precision=TOP_PRECISION)
        * score_scale_factor
    )
    fresh_key_row = jnp.dot(new_keys, key_full, preferred_element_type=jnp.float32).reshape(
        batch_rows, kv_heads, head_dimension
    )
    current_token_score = (
        jnp.einsum("phsu,phu->phs", expanded_query, fresh_key_row, precision=TOP_PRECISION)
        * score_scale_factor
    )
    new_value = jnp.dot(new_values, value_full, preferred_element_type=jnp.float32).reshape(
        batch_rows, kv_heads, head_dimension
    )
    scores = jnp.where(live_mask, scores, NEGATIVE)
    local_max = jnp.max(scores, axis=-1)
    upper_limit = jnp.maximum(lax.pmax(local_max, "seq"), current_token_score)
    softmax_terms = jnp.where(live_mask, jnp.exp(scores - upper_limit[..., None]), 0.0)
    denominator = jnp.sum(softmax_terms, axis=-1)
    totals = jnp.einsum("bkgl,blkd->bkgd", softmax_terms, rebuilt_values, precision=TOP_PRECISION)
    denominator, totals = (
        lax.psum(denominator.astype(jnp.bfloat16), "seq").astype(jnp.float32),
        lax.psum(totals.astype(jnp.bfloat16), "seq").astype(jnp.float32),
    )
    own_weight = jnp.exp(current_token_score - upper_limit)
    normalized = (totals + own_weight[..., None] * new_value[:, :, None, :]) / (
        denominator + own_weight
    )[..., None]
    normalized = normalized.reshape(batch_rows, head_count * head_dimension)
    width_local = local_head_index * head_dimension
    attended = lax.dynamic_slice_in_dim(normalized, seq_index * width_local, width_local, 1).astype(
        jnp.bfloat16
    )
    partial_out = jnp.dot(
        lax.all_gather(attended, "batch", axis=0, tiled=True),
        out_weight,
        preferred_element_type=jnp.float32,
    )
    return lax.psum_scatter(
        partial_out.astype(jnp.bfloat16), "seq", scatter_dimension=0, tiled=True
    )


def solution(mesh):
    placed = (
        P("batch", None, None),
        P("batch", "seq", None),
        P("batch", "seq", None),
        P("batch", None),
        P("batch", None),
        P("seq", None),
        P("seq", None),
        P("seq", "batch"),
        P("batch"),
    )

    def run(*args):
        chosen = fused_body if fits(mesh, args[0], args[1], args[5]) else body
        return jax.shard_map(
            chosen, mesh=mesh, in_specs=placed, out_specs=P("seq", "batch"), check_vma=False
        )(*args)

    return run
```

time: 32.1 us -> 30.6 us (0.953)
  Pallas kernels: 30.6 us -> 29.1 us
    pallas_call x1, Pallas kernels: 30.6 us -> 29.1 us  [fused_body(): pl.pallas_call(functools.partial(step_kernel, ns, nb), out_shape=jax.Shap...]
where the time goes in v1:
time: 30.6 us; the launch traced here: 30.4 us
  Pallas kernels  29.1 us (95%)
  local copies, waits for them, and re-layouts  1.29 us (4%)
    pallas_call x1, Pallas kernels, fused_body(): pl.pallas_call(functools.partial(step_kernel, ns, nb), out_shape=jax.Shap...  29.1 us
    unnamed x1, local copies, waits for them, and re-layouts  1.29 us

profile of v1, /device:TPU:0, one launch (start us, length us, event | category | flops | bytes accessed | tf_op | source)
XLA Modules:
  0.0 30.4 jit_solution(12213470808200675191)
XLA Ops:
  0.0 29.1 %decode_step.1 = bf16[16,128]{1,0:T(8,128)(2,1)} custom-call(s32[2]{0:T(128)} %lengths.1, bf16[2,64,128]{2,1,0:T(8,128)(2,1)} %query.1, bf16[2,2048,512]{2,1,0:T(8,128)(2,1)} %keys.1, bf16[2,2048,512]{2,1,0:T(8,128)(2,1)} %values.1, bf16[2,512]{1,0:T(2,128)(2,1)} %new_k.1, bf16[2,512]{1,0:T(2,128)(2,1)} %new_v.1, bf16[64,1024]{1,0:T(8,128)(2,1)} %key_up.1, ...), custom_call_target="tpu_custom_call" | custom-call | tf_op jit(solution)/shard_map/decode_step/pallas_call | solution.py:298
  29.1 1.3 %copy.12 = bf16[1,1,16,128]{3,1,2,0:T(2,128)(2,1)} copy(bf16[1,1,16,128]{3,2,1,0:T(8,128)(2,1)} %bitcast.5) | data formatting | bytes 8192

commit v2 on v1

--- a/solution.py
+++ b/solution.py
@@ -9,6 +9,8 @@
 
 NEGATIVE = -1e30
 LOG2E = 1.4426950408889634
+TINY = 1e-30
+CODES = 32767.0
 TOP_PRECISION = lax.Precision.HIGHEST
 MESH = pl.DeviceIdType.MESH
 NT = (((1,), (1,)), ((), ()))
@@ -35,9 +37,9 @@
 
 def step_kernel(
     ns, nb, lengths, query, keys, values, new_k, new_v, key_up, value_up, out_w, out,
-    kbuf, vbuf, wbuf, lens, qin, ku, vu, nk, nv, qbd, qs, rhs, score, turned_terms,
+    kbuf, vbuf, wbuf, lens, qin, ku, vu, nk, nv, qbd, qs, qscale, rhs, score, turned_terms,
     vcol, os, orecv, stats, gains, att, attf, pscr, ps, pr,
-    lsem, qsend, qrecv, vsend, vrecv, usend, urecv,
+    lsem, qsend, qrecv, csend, crecv, vsend, vrecv, usend, urecv,
     ssend, srecv, osend, orcv, asend, arcv, psend, prcv,
 ):
     me = lax.axis_index("seq")
@@ -118,7 +120,9 @@
                 b, k * group : (k + 1) * group, :
             ].astype(F32)
     asked = dot(ku[...], qbd[...].astype(BF16), NT) * (dh ** (-0.5) * LOG2E)
-    qs[me] = asked
+    largest = jnp.maximum(jnp.max(jnp.abs(asked), axis=0, keepdims=True), TINY)
+    qscale[me] = largest * (1.0 / CODES)
+    qs[me] = jnp.round(asked * (CODES / largest)).astype(jnp.int32).astype(jnp.int16)
     local[2].wait()
     own_rows = pl.ds(pl.multiple_of(mb * quarter, quarter), quarter)
     own_column = pl.ds(pl.multiple_of(me * dh, 128), dh)
@@ -127,6 +131,7 @@
     pl.semaphore_wait(barrier, ns - 1 + nb - 1)
 
     q_args = (across, "seq", lambda t: qs.at[me], lambda s: qs.at[s], qsend, qrecv)
+    c_args = (across, "seq", lambda t: qscale.at[me], lambda s: qscale.at[s], csend, crecv)
     v_args = (
         across, "seq",
         lambda t: vu.at[own_rows, pl.ds(pl.multiple_of(t * dh, 128), dh)],
@@ -142,6 +147,7 @@
         for d in order:
             receive(d, *args)
 
+    post(everyone, c_args)
     post(everyone, q_args)
     post(everyone, v_args)
 
@@ -155,7 +161,7 @@
     def gathered(half):
         for j in range(ns // 2):
             s = half * (ns // 2) + j
-            x = qs[s]
+            x = qs[s].astype(jnp.int32).astype(F32) * qscale[s]
             head = x.astype(BF16).astype(F32)
             rest = swap(x - head)
             span = pl.ds(pl.multiple_of(s * rl, rl), rl)
@@ -175,12 +181,14 @@
         )
 
     take(near, q_args)
+    take(near, c_args)
     gathered(side)
     for i in (6, 7, 3):
         local[i].wait()
     for span in spans:
         score[span, :] = half_scores(span, side)
     take(far, q_args)
+    take(far, c_args)
     gathered(1 - side)
 
     limits = jnp.where(low, lens[0], lens[1]) - me * cache_len
@@ -311,7 +319,8 @@
             vmem(new_keys.shape, BF16),
             vmem(new_values.shape, BF16),
             vmem((lanes, key_up.shape[1]), F32),
-            vmem((ns, rl, lanes), F32),
+            vmem((ns, rl, lanes), jnp.int16),
+            vmem((ns, 1, lanes), F32),
             vmem((seqs, rank, lanes), BF16),
             vmem((cache_len, lanes), F32),
             vmem((heads, cache_len), BF16),
@@ -327,7 +336,7 @@
             vmem((ns, width // 128, 128), BF16),
             dma((11,)),
         ]
-        + [dma((ns,))] * 4
+        + [dma((ns,))] * 6
         + [dma((nb,))] * 2
         + [dma((ns,))] * 2
         + [dma((seqs, ns))] * 2

time: 30.6 us -> 28.5 us (0.931)
  Pallas kernels: 29.1 us -> 27 us
    pallas_call x1, Pallas kernels: 29.1 us -> 27 us  [fused_body(): pl.pallas_call(functools.partial(step_kernel, ns, nb), out_shape=jax.Shap...]
where the time goes in v2:
time: 28.5 us; the launch traced here: 28.3 us
  Pallas kernels  27 us (95%)
  local copies, waits for them, and re-layouts  1.29 us (5%)
    pallas_call x1, Pallas kernels, fused_body(): pl.pallas_call(functools.partial(step_kernel, ns, nb), out_shape=jax.Shap...  27 us
    unnamed x1, local copies, waits for them, and re-layouts  1.29 us

profile of v2, /device:TPU:0, one launch (start us, length us, event | category | flops | bytes accessed | tf_op | source)
XLA Modules:
  0.0 28.3 jit_solution(17059144904139568736)
XLA Ops:
  0.0 27.0 %decode_step.1 = bf16[16,128]{1,0:T(8,128)(2,1)} custom-call(s32[2]{0:T(128)} %lengths.1, bf16[2,64,128]{2,1,0:T(8,128)(2,1)} %query.1, bf16[2,2048,512]{2,1,0:T(8,128)(2,1)} %keys.1, bf16[2,2048,512]{2,1,0:T(8,128)(2,1)} %values.1, bf16[2,512]{1,0:T(2,128)(2,1)} %new_k.1, bf16[2,512]{1,0:T(2,128)(2,1)} %new_v.1, bf16[64,1024]{1,0:T(8,128)(2,1)} %key_up.1, ...), custom_call_target="tpu_custom_call" | custom-call | tf_op jit(solution)/shard_map/decode_step/pallas_call | solution.py:306
  27.0 1.3 %copy.12 = bf16[1,1,16,128]{3,1,2,0:T(2,128)(2,1)} copy(bf16[1,1,16,128]{3,2,1,0:T(8,128)(2,1)} %bitcast.5) | data formatting | bytes 8192
